TPU v7x, 32 devices: a whole 2x2x4 slice. The times are simulated.
32 devices in a mesh: prow: 8 (over z, y), pcol: 4 (over x, core).
Axes of the slice: x: 2, y: 2, z: 4, core: 2. Of those that a mesh axis runs over, the one named last changes fastest.
Arguments:
- inverse_block: bfloat16 [2, 512, 512], P(None, 'prow', 'pcol'), may hold values from -1.75 to 1.75
- panel: bfloat16 [2, 512, 2048], P(None, ('prow', 'pcol')), may hold values from -0.5 to 0.5
- pattern: int32 [1, 4], replicated, may hold values 0 or 1
- diag_inverse: float32 [2, 512, 2048], P(None, None, 'pcol'), may hold values from -6 to 6
Outputs:
- offdiag: bfloat16 [2, 512, 2048], P(None, 'prow', 'pcol')
- diagonal: float32 [2, 512, 2048], P(None, None, 'pcol')
All inputs are finite; a program needn't handle non-finite values.
Results may differ from a plain program's by a relative error of at most 0.0024.
Values may be sent and summed in bfloat16 or wider, within the bound.
No kernel may reach another device: no remote copies, remote signals or barrier semaphores. Data moves between devices by JAX's collectives and lax.ppermute only.
A program may use at most 64 MiB of HBM per device.

v0:
```python
import functools

import jax
import jax.numpy as jnp
from jax import lax
from jax.experimental import pallas as pl
from jax.experimental.pallas import tpu as pltpu
from jax.sharding import PartitionSpec as P


def complex_product(left_real, left_imag, right_real, right_imag, contract):
    dims = (((contract,), (0,)), ((), ()))
    real_part = lax.dot_general(
        left_real, right_real, dims, preferred_element_type=jnp.float32
    ) - lax.dot_general(left_imag, right_imag, dims, preferred_element_type=jnp.float32)
    imag_part = lax.dot_general(
        left_real, right_imag, dims, preferred_element_type=jnp.float32
    ) + lax.dot_general(left_imag, right_real, dims, preferred_element_type=jnp.float32)
    return (real_part, imag_part)


def keep_table(pattern, row_start, row_count, col_start, col_count, block_width):
    row_ids = (row_start + jnp.arange(row_count, dtype=jnp.int32)) // block_width
    col_ids = (col_start + jnp.arange(col_count, dtype=jnp.int32)) // block_width
    row_select = (
        row_ids[:, None] == jnp.arange(pattern.shape[0], dtype=jnp.int32)[None, :]
    ).astype(jnp.float32)
    col_select = (
        col_ids[:, None] == jnp.arange(pattern.shape[1], dtype=jnp.int32)[None, :]
    ).astype(jnp.float32)
    pattern_value = pattern.astype(jnp.float32)
    row_pattern = jnp.dot(row_select, pattern_value, precision=lax.Precision.HIGHEST)
    return jnp.dot(row_pattern, col_select.T, precision=lax.Precision.HIGHEST)


def split_plan(inverse_block, panel, pattern, diag_inverse):
    WIDTH = diag_inverse.shape[1]
    rows_dev = inverse_block.shape[1]
    block_span = inverse_block.shape[2]
    fine_rows = panel.shape[1]
    columns = panel.shape[2]
    row_index = lax.axis_index("prow")
    col_index = lax.axis_index("pcol")
    col_count = lax.axis_size("pcol")
    root_count = lax.axis_size("prow") // col_count
    fine_start = (row_index * col_count + col_index) * fine_rows
    keep_mask = keep_table(pattern, fine_start, fine_rows, 0, columns, WIDTH)
    masked = jnp.where(keep_mask[None] > 0.5, panel, jnp.zeros_like(panel))
    row_panel = lax.all_gather(masked, "pcol", axis=1, tiled=True)
    flipped = jnp.swapaxes(inverse_block, 1, 2)
    split_cols = flipped.reshape(2, root_count, col_count, fine_rows, rows_dev)
    received = lax.all_to_all(split_cols, "pcol", split_axis=2, concat_axis=1, tiled=True)
    regrouped = received.reshape(2, block_span, rows_dev)
    panel_piece = lax.all_gather(masked, "prow", axis=1, tiled=True)
    part_real, part_imag = complex_product(
        regrouped[0], regrouped[1], panel_piece[0], panel_piece[1], 0
    )
    stacked = jnp.stack([part_real, part_imag])
    summed = lax.psum_scatter(stacked, "pcol", scatter_dimension=2, tiled=True)
    local_cols = summed.shape[2]
    keep_local = keep_table(
        pattern, row_index * rows_dev, rows_dev, col_index * local_cols, local_cols, WIDTH
    )
    coupled = (summed * keep_local[None]).astype(jnp.bfloat16)
    offdiag = -coupled
    block_start = col_index * local_cols // WIDTH * WIDTH
    lower_panel = lax.dynamic_slice_in_dim(row_panel, block_start, WIDTH, 2)
    diag_real, diag_imag = complex_product(
        lower_panel[0], lower_panel[1], coupled[0], coupled[1], 0
    )
    shares = lax.psum_scatter(
        jnp.stack([diag_real, diag_imag]), "prow", scatter_dimension=1, tiled=True
    )
    correction = lax.all_gather(shares, "prow", axis=1, tiled=True)
    return (offdiag, diag_inverse + correction)


def shift_perm(outer, inner, outer_step, inner_step):
    return [
        (i * inner + j, (i + outer_step) % outer * inner + (j + inner_step) % inner)
        for i in range(outer)
        for j in range(inner)
    ]


def dot(left, right, contract):
    return lax.dot_general(
        left, right, (((contract,), (0,)), ((), ())), preferred_element_type=jnp.float32
    )


def finish_kernel(
    place_ref, pattern_ref, *refs, prow, pcol, panel_count, inverse_count, width
):
    panel_refs = refs[:panel_count]
    inverse_refs = refs[panel_count : panel_count + inverse_count]
    diag_ref, offdiag_ref, out_ref, masked_ref, inv_ref, coupled_ref = refs[
        panel_count + inverse_count :
    ]
    outer, inner = prow // 2, 2
    groups = pcol // 2
    row, col = place_ref[0], place_ref[1]
    row_hi, row_lo = row // inner, row % inner
    col_hi, col_lo = col // 2, col % 2
    rows_dev = inv_ref.shape[1] // prow
    span = inv_ref.shape[2] // pcol
    fine = rows_dev // pcol
    step = pl.program_id(0)
    cols_step = out_ref.shape[2]
    block_rows = pattern_ref.shape[0]

    def source_row(dz, dy):
        return (row_hi + outer - dz) % outer * inner + (row_lo + inner - dy) % inner

    @pl.when(step == 0)
    def _():
        for dy in range(inner):
            for dz in range(outer):
                piece = panel_refs[dy * outer + dz]
                base = source_row(dz, dy) * rows_dev
                keep = pattern_ref[base // width, col * masked_ref.shape[2] // width] > 0
                for s in range(pcol):
                    at = pl.multiple_of(base + (col + pcol - s) % pcol * fine, fine)
                    values = piece[s]
                    masked_ref[:, pl.ds(at, fine), :] = jnp.where(
                        keep, values, jnp.zeros_like(values)
                    )
        pieces = []
        for ref in inverse_refs:
            pieces += [(ref, n) for n in range(ref.shape[0])]
        order = [
            (dk, dx, dy, dz)
            for dk in range(2)
            for dx in range(groups)
            for dy in range(inner)
            for dz in range(outer)
        ]
        for (ref, n), (dk, dx, dy, dz) in zip(pieces, order, strict=True):
            at_row = pl.multiple_of(source_row(dz, dy) * rows_dev, rows_dev)
            source_col = (col_hi + groups - dx) % groups * 2 + (col_lo + 2 - dk) % 2
            at_col = pl.multiple_of(source_col * span, span)
            inv_ref[:, pl.ds(at_row, rows_dev), pl.ds(at_col, span)] = ref[n]

    here = pl.ds(pl.multiple_of(step * cols_step, cols_step), cols_step)
    right_real, right_imag = masked_ref[0, :, here], masked_ref[1, :, here]
    parts = (
        dot(inv_ref[0], right_real, 1) - dot(inv_ref[1], right_imag, 1),
        dot(inv_ref[0], right_imag, 1) + dot(inv_ref[1], right_real, 1),
    )
    for part, values in enumerate(parts):
        for block in range(block_rows):
            keep = pattern_ref[block, col * masked_ref.shape[2] // width] > 0
            rows = values[block * width : (block + 1) * width]
            coupled_ref[part, block * width : (block + 1) * width, :] = jnp.where(
                keep, rows, jnp.zeros_like(rows)
            ).astype(coupled_ref.dtype)
    own = pl.ds(pl.multiple_of(row * rows_dev, rows_dev), rows_dev)
    offdiag_ref[...] = -coupled_ref[:, own, :]
    real, imag = coupled_ref[0], coupled_ref[1]
    left_real, left_imag = masked_ref[0], masked_ref[1]
    out_ref[0] = diag_ref[0] + (dot(left_real, real, 0) - dot(left_imag, imag, 0))
    out_ref[1] = diag_ref[1] + (dot(left_real, imag, 0) + dot(left_imag, real, 0))


def copy_plan(inverse_block, panel, pattern, diag_inverse):
    row = lax.axis_index("prow")
    col = lax.axis_index("pcol")
    prow = lax.axis_size("prow")
    pcol = lax.axis_size("pcol")
    width = diag_inverse.shape[1]
    local_cols = diag_inverse.shape[2]
    parts, rows_dev, span = inverse_block.shape
    outer, inner, groups = prow // 2, 2, pcol // 2

    fine_pieces = [
        lax.dynamic_slice_in_dim(panel, (col + s) % pcol * local_cols, local_cols, 2)
        for s in range(pcol)
    ]
    for s in range(1, pcol):
        fine_pieces[s] = lax.ppermute(fine_pieces[s], "pcol", shift_perm(pcol, 1, s, 0))
    mine = jnp.stack(fine_pieces)
    far = [mine] + [
        lax.ppermute(mine, "prow", shift_perm(outer, inner, dz, 0)) for dz in range(1, outer)
    ]
    near = [lax.ppermute(piece, "prow", shift_perm(outer, inner, 0, 1)) for piece in far]
    panel_pieces = far + near

    inv_own = inverse_block[None]
    column = jnp.concatenate(
        [inv_own]
        + [lax.ppermute(inv_own, "prow", shift_perm(outer, inner, dz, 0)) for dz in range(1, outer)]
    )
    rows_all = [column, lax.ppermute(column, "prow", shift_perm(outer, inner, 0, 1))]
    half = list(rows_all)
    for dx in range(1, groups):
        for piece in rows_all:
            half.append(lax.ppermute(piece, "pcol", shift_perm(groups, 2, dx, 0)))
    other = [lax.ppermute(piece, "pcol", shift_perm(groups, 2, 0, 1)) for piece in half]
    inverse_pieces = half + other

    panel_pieces = [pltpu.with_memory_space_constraint(p, pltpu.VMEM) for p in panel_pieces]
    inverse_pieces = [pltpu.with_memory_space_constraint(p, pltpu.VMEM) for p in inverse_pieces]
    order = prow * rows_dev
    steps = 2
    cols_step = local_cols // steps
    smem = pl.BlockSpec(memory_space=pltpu.SMEM)
    vmem = pl.BlockSpec(memory_space=pltpu.VMEM)
    diag_spec = pl.BlockSpec((parts, width, cols_step), lambda i: (0, 0, i))
    off_spec = pl.BlockSpec((parts, rows_dev, cols_step), lambda i: (0, 0, i))
    kernel = functools.partial(
        finish_kernel,
        prow=prow,
        pcol=pcol,
        panel_count=len(panel_pieces),
        inverse_count=len(inverse_pieces),
        width=width,
    )
    return pl.pallas_call(
        kernel,
        grid=(steps,),
        in_specs=[smem, smem] + [vmem] * (len(panel_pieces) + len(inverse_pieces)) + [diag_spec],
        out_specs=[off_spec, diag_spec],
        out_shape=[
            jax.ShapeDtypeStruct((parts, rows_dev, local_cols), panel.dtype),
            jax.ShapeDtypeStruct(diag_inverse.shape, diag_inverse.dtype),
        ],
        scratch_shapes=[
            pltpu.VMEM((parts, order, local_cols), panel.dtype),
            pltpu.VMEM((parts, order, pcol * span), panel.dtype),
            pltpu.VMEM((parts, order, cols_step), panel.dtype),
        ],
        compiler_params=pltpu.CompilerParams(dimension_semantics=("arbitrary",)),
        name="finish",
    )(jnp.stack([row, col]), pattern, *panel_pieces, *inverse_pieces, diag_inverse)


def local(inverse_block, panel, pattern, diag_inverse):
    prow = lax.axis_size("prow")
    pcol = lax.axis_size("pcol")
    parts, rows_dev, span = inverse_block.shape
    gathered = (rows_dev * prow) * (span * pcol + diag_inverse.shape[2]) * parts * 2
    room = gathered <= diag_inverse.size * 4 * 4
    whole_blocks = diag_inverse.shape[1] == diag_inverse.shape[2]
    even = prow % 2 == 0 and pcol % 2 == 0
    if room and whole_blocks and even:
        return copy_plan(inverse_block, panel, pattern, diag_inverse)
    return split_plan(inverse_block, panel, pattern, diag_inverse)


def solution(mesh):
    in_specs = (
        P(None, "prow", "pcol"),
        P(None, ("prow", "pcol"), None),
        P(),
        P(None, None, "pcol"),
    )
    out_specs = (P(None, "prow", "pcol"), P(None, None, "pcol"))
    return jax.shard_map(
        local, mesh=mesh, in_specs=in_specs, out_specs=out_specs, check_vma=False
    )
```

profile of v0, /device:TPU:0, one launch (start us, length us, event | category | flops | bytes accessed | tf_op | source)
XLA Modules:
  0.0 42.7 jit_solution(6960975306657619249)
XLA Ops:
  0.7 0.8 %dynamic-slice_bitcast_fusion = (bf16[1,2,16,512]{3,2,1,0:T(8,128)(2,1)S(1)}, bf16[2,16,512]{2,1,0:T(8,128)(2,1)S(1)}, bf16[2,16,512]{2,1,0:T(8,128)(2,1)S(1)}, bf16[2,16,512]{2,1,0:T(8,128)(2,1)S(1)}) fusion(bf16[2,16,2048]{2,1,0:T(8,128)(2,1)} %param.5, s32[]{:T(128)S(6)} %select_n.32, s32[]{:T(128)S(6)} %select_n.34, s32[]{:T(128)S(6)} %select_n.38, ...), kind=kLoop, calls=%fused_computation.2 | loop fusion | bytes 262160 | tf_op jit(solution)/shard_map/stack | solution.py:181
  1.5 0.5 %collective-permute-start = (bf16[2,16,512]{2,1,0:T(8,128)(2,1)S(1)}, bf16[2,16,512]{2,1,0:T(8,128)(2,1)S(1)}, u32[]{:S(2)}, u32[]{:S(2)}) collective-permute-start(bf16[2,16,512]{2,1,0:T(8,128)(2,1)S(1)} %get-tuple-element.3), channel_id=1, source_target_pairs={{0,1},{1,2},{2,3},{3,0},{4,5},{5,6},{6,7},{7,4},{8,9},{9,10},{10,1... | collective-permute-start | bytes 98312 | tf_op jit(solution)/shard_map/ppermute | solution.py:180
  2.1 2.0 %collective-permute-start.2 = (bf16[2,16,512]{2,1,0:T(8,128)(2,1)S(1)}, bf16[2,16,512]{2,1,0:T(8,128)(2,1)S(1)}, u32[]{:S(2)}, u32[]{:S(2)}) collective-permute-start(bf16[2,16,512]{2,1,0:T(8,128)(2,1)S(1)} %get-tuple-element.4), channel_id=1, source_target_pairs={{0,3},{1,0},{2,1},{3,2},{4,7},{5,4},{6,5},{7,6},{8,11},{9,8},{10,9... | collective-permute-start | bytes 98312 | tf_op jit(solution)/shard_map/ppermute | solution.py:180
  4.0 2.2 %collective-permute-start.1 = (bf16[2,16,512]{2,1,0:T(8,128)(2,1)S(1)}, bf16[2,16,512]{2,1,0:T(8,128)(2,1)S(1)}, u32[]{:S(2)}, u32[]{:S(2)}) collective-permute-start(bf16[2,16,512]{2,1,0:T(8,128)(2,1)S(1)} %get-tuple-element.5), channel_id=1, source_target_pairs={{0,2},{1,3},{2,0},{3,1},{4,6},{5,7},{6,4},{7,5},{8,10},{9,11},{10,... | collective-permute-start | bytes 98312 | tf_op jit(solution)/shard_map/ppermute | solution.py:180
  6.3 3.6 %collective-permute-start.12 = (bf16[1,2,64,128]{3,2,1,0:T(8,128)(2,1)}, bf16[1,2,64,128]{3,2,1,0:T(8,128)(2,1)S(1)}, u32[]{:S(2)}, u32[]{:S(2)}) collective-permute-start(bf16[1,2,64,128]{3,2,1,0:T(8,128)(2,1)} %bitcast.8), channel_id=1, source_target_pairs={{0,24},{4,28},{8,0},{12,4},{16,8},{20,12},{24,16},{28,20},{1,25},{... | collective-permute-start | bytes 98312 | tf_op jit(solution)/shard_map/ppermute | solution.py:191
  9.9 0.0 collective-permute-start.11
  9.9 0.0 collective-permute-done
  9.9 1.0 %collective-permute-start.10 = (bf16[1,2,64,128]{3,2,1,0:T(8,128)(2,1)}, bf16[1,2,64,128]{3,2,1,0:T(8,128)(2,1)S(1)}, u32[]{:S(2)}, u32[]{:S(2)}) collective-permute-start(bf16[1,2,64,128]{3,2,1,0:T(8,128)(2,1)} %bitcast.10), channel_id=1, source_target_pairs={{0,8},{4,12},{8,16},{12,20},{16,24},{20,28},{24,0},{28,4},{1,9},{5... | collective-permute-start | bytes 98312 | tf_op jit(solution)/shard_map/ppermute | solution.py:191
  10.9 0.0 collective-permute-done.2
  10.9 0.0 collective-permute-done.1
  10.9 1.6 %collective-permute-start.6 = (bf16[4,2,16,512]{3,2,1,0:T(8,128)(2,1)S(1)}, bf16[4,2,16,512]{3,2,1,0:T(8,128)(2,1)S(1)}, u32[]{:S(2)}, u32[]{:S(2)}) collective-permute-start(bf16[4,2,16,512]{3,2,1,0:T(8,128)(2,1)S(1)} %pad_maximum_fusion.refs_0_), channel_id=1, source_target_pairs={{0,4},{4,0},{8,12},{12,8},{16,20},{20,16},{24,28},{28,24},{1,5},{5... | collective-permute-start | bytes 393224 | tf_op jit(solution)/shard_map/ppermute | solution.py:185
  12.5 2.8 %collective-permute-start.5 = (bf16[4,2,16,512]{3,2,1,0:T(8,128)(2,1)S(1)}, bf16[4,2,16,512]{3,2,1,0:T(8,128)(2,1)S(1)}, u32[]{:S(2)}, u32[]{:S(2)}) collective-permute-start(bf16[4,2,16,512]{3,2,1,0:T(8,128)(2,1)S(1)} %pad_maximum_fusion.refs_0_), channel_id=1, source_target_pairs={{0,24},{4,28},{8,0},{12,4},{16,8},{20,12},{24,16},{28,20},{1,25},{... | collective-permute-start | bytes 393224 | tf_op jit(solution)/shard_map/ppermute | solution.py:183
  15.3 0.0 collective-permute-done.12
  15.3 1.1 %collective-permute-start.4 = (bf16[4,2,16,512]{3,2,1,0:T(8,128)(2,1)S(1)}, bf16[4,2,16,512]{3,2,1,0:T(8,128)(2,1)S(1)}, u32[]{:S(2)}, u32[]{:S(2)}) collective-permute-start(bf16[4,2,16,512]{3,2,1,0:T(8,128)(2,1)S(1)} %pad_maximum_fusion.refs_0_), channel_id=1, source_target_pairs={{0,16},{4,20},{8,24},{12,28},{16,0},{20,4},{24,8},{28,12},{1,17},{... | collective-permute-start | bytes 393224 | tf_op jit(solution)/shard_map/ppermute | solution.py:183
  16.5 0.0 collective-permute-done.11
  16.5 0.0 collective-permute-done.10
  16.5 0.8 %pad_maximum_fusion.1.refs_8_ = bf16[4,2,64,128]{3,2,1,0:T(8,128)(2,1)S(1)} fusion(bf16[1,2,64,128]{3,2,1,0:T(8,128)(2,1)S(1)} %collective-permute-done.12, bf16[1,2,64,128]{3,2,1,0:T(8,128)(2,1)S(1)} %collective-permute-done.11, bf16[1,2,64,128]{3,2,1,0:T(8,128)(2,1)S(1)} %collective-permute-done.10, bf16[1,2,64,128]{3,2,1,0:T(8,128)(2,1)} %bitcast.11), kind=kLoop, calls=%fused_computation.1 | loop fusion | flops 196608 | bytes 262144 | tf_op jit(solution)/shard_map/concatenate | solution.py:189
  17.2 2.1 %collective-permute-start.13 = (bf16[4,2,64,128]{3,2,1,0:T(8,128)(2,1)S(1)}, bf16[4,2,64,128]{3,2,1,0:T(8,128)(2,1)S(1)}, u32[]{:S(2)}, u32[]{:S(2)}) collective-permute-start(bf16[4,2,64,128]{3,2,1,0:T(8,128)(2,1)S(1)} %pad_maximum_fusion.1.refs_8_), channel_id=1, source_target_pairs={{0,4},{4,0},{8,12},{12,8},{16,20},{20,16},{24,28},{28,24},{1,5},{5... | collective-permute-start | bytes 393224 | tf_op jit(solution)/shard_map/ppermute | solution.py:193
  19.4 1.0 %collective-permute-start.3 = (bf16[4,2,16,512]{3,2,1,0:T(8,128)(2,1)S(1)}, bf16[4,2,16,512]{3,2,1,0:T(8,128)(2,1)S(1)}, u32[]{:S(2)}, u32[]{:S(2)}) collective-permute-start(bf16[4,2,16,512]{3,2,1,0:T(8,128)(2,1)S(1)} %pad_maximum_fusion.refs_0_), channel_id=1, source_target_pairs={{0,8},{4,12},{8,16},{12,20},{16,24},{20,28},{24,0},{28,4},{1,9},{5... | collective-permute-start | bytes 393224 | tf_op jit(solution)/shard_map/ppermute | solution.py:183
  20.3 0.0 collective-permute-done.6.refs_4_
  20.3 0.0 collective-permute-start.16
  20.3 0.0 collective-permute-done.5.refs_3_
  20.4 1.6 %collective-permute-start.14 = (bf16[4,2,64,128]{3,2,1,0:T(8,128)(2,1)S(1)}, bf16[4,2,64,128]{3,2,1,0:T(8,128)(2,1)S(1)}, u32[]{:S(2)}, u32[]{:S(2)}) collective-permute-start(bf16[4,2,64,128]{3,2,1,0:T(8,128)(2,1)S(1)} %pad_maximum_fusion.1.refs_8_), channel_id=1, source_target_pairs={{0,2},{1,3},{2,0},{3,1},{4,6},{5,7},{6,4},{7,5},{8,10},{9,11},{10,... | collective-permute-start | bytes 393224 | tf_op jit(solution)/shard_map/ppermute | solution.py:197
  22.0 4.5 %collective-permute-done.4.refs_2_ = bf16[4,2,16,512]{3,2,1,0:T(8,128)(2,1)S(1)} collective-permute-done((bf16[4,2,16,512]{3,2,1,0:T(8,128)(2,1)S(1)}, bf16[4,2,16,512]{3,2,1,0:T(8,128)(2,1)S(1)}, u32[]{:S(2)}, u32[]{:S(2)}) %collective-permute-start.4) | collective-permute-done | bytes 131104 | tf_op jit(solution)/shard_map/ppermute | solution.py:183
  26.5 0.5 %collective-permute-start.9 = (bf16[4,2,16,512]{3,2,1,0:T(8,128)(2,1)S(1)}, bf16[4,2,16,512]{3,2,1,0:T(8,128)(2,1)S(1)}, u32[]{:S(2)}, u32[]{:S(2)}) collective-permute-start(bf16[4,2,16,512]{3,2,1,0:T(8,128)(2,1)S(1)} %collective-permute-done.5.refs_3_), channel_id=1, source_target_pairs={{0,4},{4,0},{8,12},{12,8},{16,20},{20,16},{24,28},{28,24},{1,5},{5... | collective-permute-start | bytes 393224 | tf_op jit(solution)/shard_map/ppermute | solution.py:185
  27.0 0.0 collective-permute-done.13.refs_9_
  27.0 1.5 %collective-permute-start.15 = (bf16[4,2,64,128]{3,2,1,0:T(8,128)(2,1)S(1)}, bf16[4,2,64,128]{3,2,1,0:T(8,128)(2,1)S(1)}, u32[]{:S(2)}, u32[]{:S(2)}) collective-permute-start(bf16[4,2,64,128]{3,2,1,0:T(8,128)(2,1)S(1)} %collective-permute-done.13.refs_9_), channel_id=1, source_target_pairs={{0,2},{1,3},{2,0},{3,1},{4,6},{5,7},{6,4},{7,5},{8,10},{9,11},{10,... | collective-permute-start | bytes 393224 | tf_op jit(solution)/shard_map/ppermute | solution.py:197
  28.5 0.0 collective-permute-done.3.refs_1_
  28.5 0.0 collective-permute-start.17
  28.5 0.0 collective-permute-done.16.refs_12_
  28.5 1.2 %collective-permute-start.8 = (bf16[4,2,16,512]{3,2,1,0:T(8,128)(2,1)S(1)}, bf16[4,2,16,512]{3,2,1,0:T(8,128)(2,1)S(1)}, u32[]{:S(2)}, u32[]{:S(2)}) collective-permute-start(bf16[4,2,16,512]{3,2,1,0:T(8,128)(2,1)S(1)} %collective-permute-done.4.refs_2_), channel_id=1, source_target_pairs={{0,4},{4,0},{8,12},{12,8},{16,20},{20,16},{24,28},{28,24},{1,5},{5... | collective-permute-start | bytes 393224 | tf_op jit(solution)/shard_map/ppermute | solution.py:185
  29.7 0.0 collective-permute-done.14.refs_10_
  29.7 0.9 %collective-permute-start.7 = (bf16[4,2,16,512]{3,2,1,0:T(8,128)(2,1)S(1)}, bf16[4,2,16,512]{3,2,1,0:T(8,128)(2,1)S(1)}, u32[]{:S(2)}, u32[]{:S(2)}) collective-permute-start(bf16[4,2,16,512]{3,2,1,0:T(8,128)(2,1)S(1)} %collective-permute-done.3.refs_1_), channel_id=1, source_target_pairs={{0,4},{4,0},{8,12},{12,8},{16,20},{20,16},{24,28},{28,24},{1,5},{5... | collective-permute-start | bytes 393224 | tf_op jit(solution)/shard_map/ppermute | solution.py:185
  30.6 0.9 %collective-permute-done.9.refs_7_ = bf16[4,2,16,512]{3,2,1,0:T(8,128)(2,1)S(1)} collective-permute-done((bf16[4,2,16,512]{3,2,1,0:T(8,128)(2,1)S(1)}, bf16[4,2,16,512]{3,2,1,0:T(8,128)(2,1)S(1)}, u32[]{:S(2)}, u32[]{:S(2)}) %collective-permute-start.9) | collective-permute-done | bytes 131104 | tf_op jit(solution)/shard_map/ppermute | solution.py:185
  31.4 0.0 collective-permute-start.18
  31.4 0.5 %collective-permute-done.15.refs_11_ = bf16[4,2,64,128]{3,2,1,0:T(8,128)(2,1)S(1)} collective-permute-done((bf16[4,2,64,128]{3,2,1,0:T(8,128)(2,1)S(1)}, bf16[4,2,64,128]{3,2,1,0:T(8,128)(2,1)S(1)}, u32[]{:S(2)}, u32[]{:S(2)}) %collective-permute-start.15) | collective-permute-done | bytes 131104 | tf_op jit(solution)/shard_map/ppermute | solution.py:197
  31.9 0.0 collective-permute-start.19
  32.0 0.6 %pad_add_fusion.place_ref = s32[2]{0:T(128)} fusion(s32[1]{0:T(128)} %bitcast.1, s32[1]{0:T(128)} %bitcast), kind=kLoop, calls=%fused_computation.6 | loop fusion | flops 2 | bytes 16 | tf_op jit(solution)/shard_map/stack | solution.py:234
  32.5 2.4 %collective-permute-done.8.refs_6_ = bf16[4,2,16,512]{3,2,1,0:T(8,128)(2,1)S(1)} collective-permute-done((bf16[4,2,16,512]{3,2,1,0:T(8,128)(2,1)S(1)}, bf16[4,2,16,512]{3,2,1,0:T(8,128)(2,1)S(1)}, u32[]{:S(2)}, u32[]{:S(2)}) %collective-permute-start.8) | collective-permute-done | bytes 131104 | tf_op jit(solution)/shard_map/ppermute | solution.py:185
  34.9 2.3 %collective-permute-done.7.refs_5_ = bf16[4,2,16,512]{3,2,1,0:T(8,128)(2,1)S(1)} collective-permute-done((bf16[4,2,16,512]{3,2,1,0:T(8,128)(2,1)S(1)}, bf16[4,2,16,512]{3,2,1,0:T(8,128)(2,1)S(1)}, u32[]{:S(2)}, u32[]{:S(2)}) %collective-permute-start.7) | collective-permute-done | bytes 131104 | tf_op jit(solution)/shard_map/ppermute | solution.py:185
  37.2 0.0 collective-permute-done.18.refs_14_
  37.2 0.0 collective-permute-done.17.refs_13_
  37.2 0.0 collective-permute-done.19.refs_15_
  37.2 5.5 %finish.1 = (bf16[2,64,512]{2,1,0:T(8,128)(2,1)}, f32[2,512,512]{2,1,0:T(8,128)}) custom-call(s32[2]{0:T(128)} %pad_add_fusion.place_ref, s32[1,4]{1,0:T(1,128)} %pattern_ref.1, bf16[4,2,16,512]{3,2,1,0:T(8,128)(2,1)S(1)} %pad_maximum_fusion.refs_0_, bf16[4,2,16,512]{3,2,1,0:T(8,128)(2,1)S(1)} %collective-permute-done.3.refs_1_, ...), custom_call_target="tpu_custom_call" | custom-call | tf_op jit(solution)/shard_map/finish/pallas_call | solution.py:218
  (1 shorter events, 0.0 us)
Async XLA Ops:
  1.5 8.4 %collective-permute-start = (bf16[2,16,512]{2,1,0:T(8,128)(2,1)S(1)}, bf16[2,16,512]{2,1,0:T(8,128)(2,1)S(1)}, u32[]{:S(2)}, u32[]{:S(2)}) collective-permute-start(bf16[2,16,512]{2,1,0:T(8,128)(2,1)S(1)} %get-tuple-element.3), channel_id=1, source_target_pairs={{0,1},{1,2},{2,3},{3,0},{4,5},{5,6},{6,7},{7,4},{8,9},{9,10},{10,1... | collective-permute-start | bytes 98312 | tf_op jit(solution)/shard_map/ppermute | solution.py:180
  2.1 8.8 %collective-permute-start.2 = (bf16[2,16,512]{2,1,0:T(8,128)(2,1)S(1)}, bf16[2,16,512]{2,1,0:T(8,128)(2,1)S(1)}, u32[]{:S(2)}, u32[]{:S(2)}) collective-permute-start(bf16[2,16,512]{2,1,0:T(8,128)(2,1)S(1)} %get-tuple-element.4), channel_id=1, source_target_pairs={{0,3},{1,0},{2,1},{3,2},{4,7},{5,4},{6,5},{7,6},{8,11},{9,8},{10,9... | collective-permute-start | bytes 98312 | tf_op jit(solution)/shard_map/ppermute | solution.py:180
  4.0 6.9 %collective-permute-start.1 = (bf16[2,16,512]{2,1,0:T(8,128)(2,1)S(1)}, bf16[2,16,512]{2,1,0:T(8,128)(2,1)S(1)}, u32[]{:S(2)}, u32[]{:S(2)}) collective-permute-start(bf16[2,16,512]{2,1,0:T(8,128)(2,1)S(1)} %get-tuple-element.5), channel_id=1, source_target_pairs={{0,2},{1,3},{2,0},{3,1},{4,6},{5,7},{6,4},{7,5},{8,10},{9,11},{10,... | collective-permute-start | bytes 98312 | tf_op jit(solution)/shard_map/ppermute | solution.py:180
  6.3 9.1 %collective-permute-start.12 = (bf16[1,2,64,128]{3,2,1,0:T(8,128)(2,1)}, bf16[1,2,64,128]{3,2,1,0:T(8,128)(2,1)S(1)}, u32[]{:S(2)}, u32[]{:S(2)}) collective-permute-start(bf16[1,2,64,128]{3,2,1,0:T(8,128)(2,1)} %bitcast.8), channel_id=1, source_target_pairs={{0,24},{4,28},{8,0},{12,4},{16,8},{20,12},{24,16},{28,20},{1,25},{... | collective-permute-start | bytes 98312 | tf_op jit(solution)/shard_map/ppermute | solution.py:191
  9.9 6.6 %collective-permute-start.11 = (bf16[1,2,64,128]{3,2,1,0:T(8,128)(2,1)}, bf16[1,2,64,128]{3,2,1,0:T(8,128)(2,1)S(1)}, u32[]{:S(2)}, u32[]{:S(2)}) collective-permute-start(bf16[1,2,64,128]{3,2,1,0:T(8,128)(2,1)} %bitcast.9), channel_id=1, source_target_pairs={{0,16},{4,20},{8,24},{12,28},{16,0},{20,4},{24,8},{28,12},{1,17},{... | collective-permute-start | bytes 98312 | tf_op jit(solution)/shard_map/ppermute | solution.py:191
  9.9 6.6 %collective-permute-start.10 = (bf16[1,2,64,128]{3,2,1,0:T(8,128)(2,1)}, bf16[1,2,64,128]{3,2,1,0:T(8,128)(2,1)S(1)}, u32[]{:S(2)}, u32[]{:S(2)}) collective-permute-start(bf16[1,2,64,128]{3,2,1,0:T(8,128)(2,1)} %bitcast.10), channel_id=1, source_target_pairs={{0,8},{4,12},{8,16},{12,20},{16,24},{20,28},{24,0},{28,4},{1,9},{5... | collective-permute-start | bytes 98312 | tf_op jit(solution)/shard_map/ppermute | solution.py:191
  10.9 9.4 %collective-permute-start.6 = (bf16[4,2,16,512]{3,2,1,0:T(8,128)(2,1)S(1)}, bf16[4,2,16,512]{3,2,1,0:T(8,128)(2,1)S(1)}, u32[]{:S(2)}, u32[]{:S(2)}) collective-permute-start(bf16[4,2,16,512]{3,2,1,0:T(8,128)(2,1)S(1)} %pad_maximum_fusion.refs_0_), channel_id=1, source_target_pairs={{0,4},{4,0},{8,12},{12,8},{16,20},{20,16},{24,28},{28,24},{1,5},{5... | collective-permute-start | bytes 393224 | tf_op jit(solution)/shard_map/ppermute | solution.py:185
  12.5 7.8 %collective-permute-start.5 = (bf16[4,2,16,512]{3,2,1,0:T(8,128)(2,1)S(1)}, bf16[4,2,16,512]{3,2,1,0:T(8,128)(2,1)S(1)}, u32[]{:S(2)}, u32[]{:S(2)}) collective-permute-start(bf16[4,2,16,512]{3,2,1,0:T(8,128)(2,1)S(1)} %pad_maximum_fusion.refs_0_), channel_id=1, source_target_pairs={{0,24},{4,28},{8,0},{12,4},{16,8},{20,12},{24,16},{28,20},{1,25},{... | collective-permute-start | bytes 393224 | tf_op jit(solution)/shard_map/ppermute | solution.py:183
  15.3 11.1 %collective-permute-start.4 = (bf16[4,2,16,512]{3,2,1,0:T(8,128)(2,1)S(1)}, bf16[4,2,16,512]{3,2,1,0:T(8,128)(2,1)S(1)}, u32[]{:S(2)}, u32[]{:S(2)}) collective-permute-start(bf16[4,2,16,512]{3,2,1,0:T(8,128)(2,1)S(1)} %pad_maximum_fusion.refs_0_), channel_id=1, source_target_pairs={{0,16},{4,20},{8,24},{12,28},{16,0},{20,4},{24,8},{28,12},{1,17},{... | collective-permute-start | bytes 393224 | tf_op jit(solution)/shard_map/ppermute | solution.py:183
  17.2 9.7 %collective-permute-start.13 = (bf16[4,2,64,128]{3,2,1,0:T(8,128)(2,1)S(1)}, bf16[4,2,64,128]{3,2,1,0:T(8,128)(2,1)S(1)}, u32[]{:S(2)}, u32[]{:S(2)}) collective-permute-start(bf16[4,2,64,128]{3,2,1,0:T(8,128)(2,1)S(1)} %pad_maximum_fusion.1.refs_8_), channel_id=1, source_target_pairs={{0,4},{4,0},{8,12},{12,8},{16,20},{20,16},{24,28},{28,24},{1,5},{5... | collective-permute-start | bytes 393224 | tf_op jit(solution)/shard_map/ppermute | solution.py:193
  19.4 9.1 %collective-permute-start.3 = (bf16[4,2,16,512]{3,2,1,0:T(8,128)(2,1)S(1)}, bf16[4,2,16,512]{3,2,1,0:T(8,128)(2,1)S(1)}, u32[]{:S(2)}, u32[]{:S(2)}) collective-permute-start(bf16[4,2,16,512]{3,2,1,0:T(8,128)(2,1)S(1)} %pad_maximum_fusion.refs_0_), channel_id=1, source_target_pairs={{0,8},{4,12},{8,16},{12,20},{16,24},{20,28},{24,0},{28,4},{1,9},{5... | collective-permute-start | bytes 393224 | tf_op jit(solution)/shard_map/ppermute | solution.py:183
  20.3 8.1 %collective-permute-start.16 = (bf16[4,2,64,128]{3,2,1,0:T(8,128)(2,1)S(1)}, bf16[4,2,64,128]{3,2,1,0:T(8,128)(2,1)S(1)}, u32[]{:S(2)}, u32[]{:S(2)}) collective-permute-start(bf16[4,2,64,128]{3,2,1,0:T(8,128)(2,1)S(1)} %pad_maximum_fusion.1.refs_8_), channel_id=1, source_target_pairs={{0,1},{1,0},{2,3},{3,2},{4,5},{5,4},{6,7},{7,6},{8,9},{9,8},{10,11... | collective-permute-start | bytes 393224 | tf_op jit(solution)/shard_map/ppermute | solution.py:198
  20.4 9.4 %collective-permute-start.14 = (bf16[4,2,64,128]{3,2,1,0:T(8,128)(2,1)S(1)}, bf16[4,2,64,128]{3,2,1,0:T(8,128)(2,1)S(1)}, u32[]{:S(2)}, u32[]{:S(2)}) collective-permute-start(bf16[4,2,64,128]{3,2,1,0:T(8,128)(2,1)S(1)} %pad_maximum_fusion.1.refs_8_), channel_id=1, source_target_pairs={{0,2},{1,3},{2,0},{3,1},{4,6},{5,7},{6,4},{7,5},{8,10},{9,11},{10,... | collective-permute-start | bytes 393224 | tf_op jit(solution)/shard_map/ppermute | solution.py:197
  26.5 5.0 %collective-permute-start.9 = (bf16[4,2,16,512]{3,2,1,0:T(8,128)(2,1)S(1)}, bf16[4,2,16,512]{3,2,1,0:T(8,128)(2,1)S(1)}, u32[]{:S(2)}, u32[]{:S(2)}) collective-permute-start(bf16[4,2,16,512]{3,2,1,0:T(8,128)(2,1)S(1)} %collective-permute-done.5.refs_3_), channel_id=1, source_target_pairs={{0,4},{4,0},{8,12},{12,8},{16,20},{20,16},{24,28},{28,24},{1,5},{5... | collective-permute-start | bytes 393224 | tf_op jit(solution)/shard_map/ppermute | solution.py:185
  27.0 5.0 %collective-permute-start.15 = (bf16[4,2,64,128]{3,2,1,0:T(8,128)(2,1)S(1)}, bf16[4,2,64,128]{3,2,1,0:T(8,128)(2,1)S(1)}, u32[]{:S(2)}, u32[]{:S(2)}) collective-permute-start(bf16[4,2,64,128]{3,2,1,0:T(8,128)(2,1)S(1)} %collective-permute-done.13.refs_9_), channel_id=1, source_target_pairs={{0,2},{1,3},{2,0},{3,1},{4,6},{5,7},{6,4},{7,5},{8,10},{9,11},{10,... | collective-permute-start | bytes 393224 | tf_op jit(solution)/shard_map/ppermute | solution.py:197
  28.5 8.7 %collective-permute-start.17 = (bf16[4,2,64,128]{3,2,1,0:T(8,128)(2,1)S(1)}, bf16[4,2,64,128]{3,2,1,0:T(8,128)(2,1)S(1)}, u32[]{:S(2)}, u32[]{:S(2)}) collective-permute-start(bf16[4,2,64,128]{3,2,1,0:T(8,128)(2,1)S(1)} %collective-permute-done.13.refs_9_), channel_id=1, source_target_pairs={{0,1},{1,0},{2,3},{3,2},{4,5},{5,4},{6,7},{7,6},{8,9},{9,8},{10,11... | collective-permute-start | bytes 393224 | tf_op jit(solution)/shard_map/ppermute | solution.py:198
  28.5 6.4 %collective-permute-start.8 = (bf16[4,2,16,512]{3,2,1,0:T(8,128)(2,1)S(1)}, bf16[4,2,16,512]{3,2,1,0:T(8,128)(2,1)S(1)}, u32[]{:S(2)}, u32[]{:S(2)}) collective-permute-start(bf16[4,2,16,512]{3,2,1,0:T(8,128)(2,1)S(1)} %collective-permute-done.4.refs_2_), channel_id=1, source_target_pairs={{0,4},{4,0},{8,12},{12,8},{16,20},{20,16},{24,28},{28,24},{1,5},{5... | collective-permute-start | bytes 393224 | tf_op jit(solution)/shard_map/ppermute | solution.py:185
  29.7 7.5 %collective-permute-start.7 = (bf16[4,2,16,512]{3,2,1,0:T(8,128)(2,1)S(1)}, bf16[4,2,16,512]{3,2,1,0:T(8,128)(2,1)S(1)}, u32[]{:S(2)}, u32[]{:S(2)}) collective-permute-start(bf16[4,2,16,512]{3,2,1,0:T(8,128)(2,1)S(1)} %collective-permute-done.3.refs_1_), channel_id=1, source_target_pairs={{0,4},{4,0},{8,12},{12,8},{16,20},{20,16},{24,28},{28,24},{1,5},{5... | collective-permute-start | bytes 393224 | tf_op jit(solution)/shard_map/ppermute | solution.py:185
  31.4 5.8 %collective-permute-start.18 = (bf16[4,2,64,128]{3,2,1,0:T(8,128)(2,1)S(1)}, bf16[4,2,64,128]{3,2,1,0:T(8,128)(2,1)S(1)}, u32[]{:S(2)}, u32[]{:S(2)}) collective-permute-start(bf16[4,2,64,128]{3,2,1,0:T(8,128)(2,1)S(1)} %collective-permute-done.14.refs_10_), channel_id=1, source_target_pairs={{0,1},{1,0},{2,3},{3,2},{4,5},{5,4},{6,7},{7,6},{8,9},{9,8},{10,11... | collective-permute-start | bytes 393224 | tf_op jit(solution)/shard_map/ppermute | solution.py:198
  31.9 5.3 %collective-permute-start.19 = (bf16[4,2,64,128]{3,2,1,0:T(8,128)(2,1)S(1)}, bf16[4,2,64,128]{3,2,1,0:T(8,128)(2,1)S(1)}, u32[]{:S(2)}, u32[]{:S(2)}) collective-permute-start(bf16[4,2,64,128]{3,2,1,0:T(8,128)(2,1)S(1)} %collective-permute-done.15.refs_11_), channel_id=1, source_target_pairs={{0,1},{1,0},{2,3},{3,2},{4,5},{5,4},{6,7},{7,6},{8,9},{9,8},{10,11... | collective-permute-start | bytes 393224 | tf_op jit(solution)/shard_map/ppermute | solution.py:198
where the time goes:
time: 42.9 us; the launch traced here: 42.7 us
  starting transfers between devices  23.7 us (55%)
  waiting for transfers between devices  10.6 us (25%)
  Pallas kernels  5.45 us (13%)
  other arithmetic  1.38 us (3%)
  local copies, waits for them, and re-layouts  0.83 us (2%)
  between operations  0.73 us (2%)
    ppermute x4, waiting for transfers between devices, copy_plan(): lax.ppermute(piece, 'prow', shift_perm(outer, inner, 0, 1))  5.52 us
    pallas_call x1, Pallas kernels, copy_plan(): pl.pallas_call(kernel, grid=(steps,), in_specs=[smem, smem] + [vmem] * (l...  5.45 us
    ppermute x3, starting transfers between devices, copy_plan(): lax.ppermute(mine, 'prow', shift_perm(outer, inner, dz, 0))  4.89 us
    ppermute x3, starting transfers between devices, copy_plan(): lax.ppermute(fine_pieces[s], 'pcol', shift_perm(pcol, 1, s, 0))  4.76 us
    ppermute x3, starting transfers between devices, copy_plan(): lax.ppermute(inv_own, 'prow', shift_perm(outer, inner, dz, 0))  4.62 us
    ppermute x3, waiting for transfers between devices, copy_plan(): lax.ppermute(mine, 'prow', shift_perm(outer, inner, dz, 0))  4.5 us
    ppermute x4, starting transfers between devices, copy_plan(): lax.ppermute(piece, 'prow', shift_perm(outer, inner, 0, 1))  4.18 us
    ppermute x2, starting transfers between devices, copy_plan(): half.append(lax.ppermute(piece, 'pcol', shift_perm(groups, 2, dx, 0)))  3.12 us
  transfers between devices with their start and end apart: 20, of which 5 were waited for; matrix products, arithmetic and copies ran while one was open for 3% of the time, Pallas kernels for 0%

commit v1 on v0

--- a/solution.py
+++ b/solution.py
@@ -75,9 +75,25 @@
     return (offdiag, diag_inverse + correction)
 
 
-def shift_perm(outer, inner, outer_step, inner_step):
+def is_power(count):
+    return count & (count - 1) == 0
+
+
+def step_from(place, step, count):
+    if is_power(count):
+        return place ^ step
+    return (place + count - step) % count
+
+
+def step_to(place, step, count):
+    if is_power(count):
+        return place ^ step
+    return (place + step) % count
+
+
+def step_perm(outer, inner, outer_step, inner_step):
     return [
-        (i * inner + j, (i + outer_step) % outer * inner + (j + inner_step) % inner)
+        (i * inner + j, step_to(i, outer_step, outer) * inner + step_to(j, inner_step, inner))
         for i in range(outer)
         for j in range(inner)
     ]
@@ -90,16 +106,16 @@
 
 
 def finish_kernel(
-    place_ref, pattern_ref, *refs, prow, pcol, panel_count, inverse_count, width
+    row_ref, col_ref, pattern_ref, *refs, prow, pcol, panel_count, inverse_count, width
 ):
     panel_refs = refs[:panel_count]
     inverse_refs = refs[panel_count : panel_count + inverse_count]
-    diag_ref, offdiag_ref, out_ref, masked_ref, inv_ref, coupled_ref = refs[
+    diag_ref, offdiag_ref, out_ref, masked_ref, turned_ref, inv_ref, coupled_ref = refs[
         panel_count + inverse_count :
     ]
     outer, inner = prow // 2, 2
     groups = pcol // 2
-    row, col = place_ref[0], place_ref[1]
+    row, col = row_ref[0], col_ref[0]
     row_hi, row_lo = row // inner, row % inner
     col_hi, col_lo = col // 2, col % 2
     rows_dev = inv_ref.shape[1] // prow
@@ -110,7 +126,7 @@
     block_rows = pattern_ref.shape[0]
 
     def source_row(dz, dy):
-        return (row_hi + outer - dz) % outer * inner + (row_lo + inner - dy) % inner
+        return step_from(row_hi, dz, outer) * inner + step_from(row_lo, dy, inner)
 
     @pl.when(step == 0)
     def _():
@@ -120,7 +136,7 @@
                 base = source_row(dz, dy) * rows_dev
                 keep = pattern_ref[base // width, col * masked_ref.shape[2] // width] > 0
                 for s in range(pcol):
-                    at = pl.multiple_of(base + (col + pcol - s) % pcol * fine, fine)
+                    at = pl.multiple_of(base + step_from(col, s, pcol) * fine, fine)
                     values = piece[s]
                     masked_ref[:, pl.ds(at, fine), :] = jnp.where(
                         keep, values, jnp.zeros_like(values)
@@ -137,9 +153,11 @@
         ]
         for (ref, n), (dk, dx, dy, dz) in zip(pieces, order, strict=True):
             at_row = pl.multiple_of(source_row(dz, dy) * rows_dev, rows_dev)
-            source_col = (col_hi + groups - dx) % groups * 2 + (col_lo + 2 - dk) % 2
+            source_col = step_from(col_hi, dx, groups) * 2 + step_from(col_lo, dk, 2)
             at_col = pl.multiple_of(source_col * span, span)
             inv_ref[:, pl.ds(at_row, rows_dev), pl.ds(at_col, span)] = ref[n]
+        for part in range(2):
+            turned_ref[part] = masked_ref[part].T
 
     here = pl.ds(pl.multiple_of(step * cols_step, cols_step), cols_step)
     right_real, right_imag = masked_ref[0, :, here], masked_ref[1, :, here]
@@ -157,9 +175,9 @@
     own = pl.ds(pl.multiple_of(row * rows_dev, rows_dev), rows_dev)
     offdiag_ref[...] = -coupled_ref[:, own, :]
     real, imag = coupled_ref[0], coupled_ref[1]
-    left_real, left_imag = masked_ref[0], masked_ref[1]
-    out_ref[0] = diag_ref[0] + (dot(left_real, real, 0) - dot(left_imag, imag, 0))
-    out_ref[1] = diag_ref[1] + (dot(left_real, imag, 0) + dot(left_imag, real, 0))
+    left_real, left_imag = turned_ref[0], turned_ref[1]
+    out_ref[0] = diag_ref[0] + (dot(left_real, real, 1) - dot(left_imag, imag, 1))
+    out_ref[1] = diag_ref[1] + (dot(left_real, imag, 1) + dot(left_imag, real, 1))
 
 
 def copy_plan(inverse_block, panel, pattern, diag_inverse):
@@ -173,35 +191,35 @@
     outer, inner, groups = prow // 2, 2, pcol // 2
 
     fine_pieces = [
-        lax.dynamic_slice_in_dim(panel, (col + s) % pcol * local_cols, local_cols, 2)
+        lax.dynamic_slice_in_dim(panel, step_to(col, s, pcol) * local_cols, local_cols, 2)
         for s in range(pcol)
     ]
     for s in range(1, pcol):
-        fine_pieces[s] = lax.ppermute(fine_pieces[s], "pcol", shift_perm(pcol, 1, s, 0))
+        fine_pieces[s] = lax.ppermute(fine_pieces[s], "pcol", step_perm(pcol, 1, s, 0))
     mine = jnp.stack(fine_pieces)
     far = [mine] + [
-        lax.ppermute(mine, "prow", shift_perm(outer, inner, dz, 0)) for dz in range(1, outer)
-    ]
-    near = [lax.ppermute(piece, "prow", shift_perm(outer, inner, 0, 1)) for piece in far]
+        lax.ppermute(mine, "prow", step_perm(outer, inner, dz, 0)) for dz in range(1, outer)
+    ]
+    near = [lax.ppermute(piece, "prow", step_perm(outer, inner, 0, 1)) for piece in far]
     panel_pieces = far + near
 
     inv_own = inverse_block[None]
     column = jnp.concatenate(
         [inv_own]
-        + [lax.ppermute(inv_own, "prow", shift_perm(outer, inner, dz, 0)) for dz in range(1, outer)]
-    )
-    rows_all = [column, lax.ppermute(column, "prow", shift_perm(outer, inner, 0, 1))]
+        + [lax.ppermute(inv_own, "prow", step_perm(outer, inner, dz, 0)) for dz in range(1, outer)]
+    )
+    rows_all = [column, lax.ppermute(column, "prow", step_perm(outer, inner, 0, 1))]
     half = list(rows_all)
     for dx in range(1, groups):
         for piece in rows_all:
-            half.append(lax.ppermute(piece, "pcol", shift_perm(groups, 2, dx, 0)))
-    other = [lax.ppermute(piece, "pcol", shift_perm(groups, 2, 0, 1)) for piece in half]
+            half.append(lax.ppermute(piece, "pcol", step_perm(groups, 2, dx, 0)))
+    other = [lax.ppermute(piece, "pcol", step_perm(groups, 2, 0, 1)) for piece in half]
     inverse_pieces = half + other
 
     panel_pieces = [pltpu.with_memory_space_constraint(p, pltpu.VMEM) for p in panel_pieces]
     inverse_pieces = [pltpu.with_memory_space_constraint(p, pltpu.VMEM) for p in inverse_pieces]
     order = prow * rows_dev
-    steps = 2
+    steps = local_cols // 128
     cols_step = local_cols // steps
     smem = pl.BlockSpec(memory_space=pltpu.SMEM)
     vmem = pl.BlockSpec(memory_space=pltpu.VMEM)
@@ -218,7 +236,7 @@
     return pl.pallas_call(
         kernel,
         grid=(steps,),
-        in_specs=[smem, smem] + [vmem] * (len(panel_pieces) + len(inverse_pieces)) + [diag_spec],
+        in_specs=[smem, smem, smem] + [vmem] * (len(panel_pieces) + len(inverse_pieces)) + [diag_spec],
         out_specs=[off_spec, diag_spec],
         out_shape=[
             jax.ShapeDtypeStruct((parts, rows_dev, local_cols), panel.dtype),
@@ -226,12 +244,13 @@
         ],
         scratch_shapes=[
             pltpu.VMEM((parts, order, local_cols), panel.dtype),
+            pltpu.VMEM((parts, local_cols, order), panel.dtype),
             pltpu.VMEM((parts, order, pcol * span), panel.dtype),
             pltpu.VMEM((parts, order, cols_step), panel.dtype),
         ],
         compiler_params=pltpu.CompilerParams(dimension_semantics=("arbitrary",)),
         name="finish",
-    )(jnp.stack([row, col]), pattern, *panel_pieces, *inverse_pieces, diag_inverse)
+    )(row.reshape(1), col.reshape(1), pattern, *panel_pieces, *inverse_pieces, diag_inverse)
 
 
 def local(inverse_block, panel, pattern, diag_inverse):
@@ -240,9 +259,11 @@
     parts, rows_dev, span = inverse_block.shape
     gathered = (rows_dev * prow) * (span * pcol + diag_inverse.shape[2]) * parts * 2
     room = gathered <= diag_inverse.size * 4 * 4
+    aligned = diag_inverse.shape[1] % rows_dev == 0 and rows_dev % (16 * pcol) == 0
+    aligned = aligned and span % 128 == 0 and diag_inverse.shape[2] % 128 == 0
     whole_blocks = diag_inverse.shape[1] == diag_inverse.shape[2]
     even = prow % 2 == 0 and pcol % 2 == 0
-    if room and whole_blocks and even:
+    if room and whole_blocks and even and aligned:
         return copy_plan(inverse_block, panel, pattern, diag_inverse)
     return split_plan(inverse_block, panel, pattern, diag_inverse)
 

time: 42.9 us -> 45.9 us (1.070)
  Pallas kernels: 5.45 us -> 9.46 us
  waiting for transfers between devices: 10.6 us -> 8.32 us
  starting transfers between devices: 23.7 us -> 25.5 us
  other arithmetic: 1.38 us -> 0.8 us
    pallas_call x1, Pallas kernels: 5.45 us -> 9.46 us  [copy_plan(): pl.pallas_call(kernel, grid=(steps,), in_specs=[smem, smem, smem] + [vmem...]
    ppermute x20, waiting for transfers between devices: 10.6 us -> 8.32 us  [the longest x4 5.71 us: copy_plan(): lax.ppermute(piece, 'prow', step_perm(outer, inner, 0, 1))]
    ppermute x20, starting transfers between devices: 23.7 us -> 25.5 us  [the longest x1 6.16 us: copy_plan(): lax.ppermute(column, 'prow', step_perm(outer, inner, 0, 1))]
    another operation x1 -> x0, other arithmetic: 0.58 us -> none  [copy_plan(): jnp.stack([row, col])]
  transfers between devices with their start and end apart: 20 -> 20, of which waited for: 5 -> 5; matrix products, arithmetic and copies ran while one was open for 3% -> 2% of each run, Pallas kernels for 0% -> 0%
where the time goes in v1:
time: 45.9 us; the launch traced here: 45.6 us
  starting transfers between devices  25.5 us (56%)
  Pallas kernels  9.46 us (21%)
  waiting for transfers between devices  8.32 us (18%)
  local copies, waits for them, and re-layouts  0.83 us (2%)
  other arithmetic  0.8 us (2%)
  between operations  0.71 us (2%)
    pallas_call x1, Pallas kernels, copy_plan(): pl.pallas_call(kernel, grid=(steps,), in_specs=[smem, smem, smem] + [vmem...  9.46 us
    ppermute x1, starting transfers between devices, copy_plan(): lax.ppermute(column, 'prow', step_perm(outer, inner, 0, 1))  6.16 us
    ppermute x4, waiting for transfers between devices, copy_plan(): lax.ppermute(piece, 'prow', step_perm(outer, inner, 0, 1))  5.71 us
    ppermute x4, starting transfers between devices, copy_plan(): lax.ppermute(piece, 'prow', step_perm(outer, inner, 0, 1))  4.8 us
    ppermute x3, starting transfers between devices, copy_plan(): lax.ppermute(inv_own, 'prow', step_perm(outer, inner, dz, 0))  4.66 us
    ppermute x3, starting transfers between devices, copy_plan(): lax.ppermute(mine, 'prow', step_perm(outer, inner, dz, 0))  3.61 us
    ppermute x3, starting transfers between devices, copy_plan(): lax.ppermute(fine_pieces[s], 'pcol', step_perm(pcol, 1, s, 0))  3.19 us
    ppermute x2, starting transfers between devices, copy_plan(): half.append(lax.ppermute(piece, 'pcol', step_perm(groups, 2, dx, 0)))  3.05 us
  transfers between devices with their start and end apart: 20, of which 5 were waited for; matrix products, arithmetic and copies ran while one was open for 2% of the time, Pallas kernels for 0%

profile of v1, /device:TPU:0, one launch (start us, length us, event | category | flops | bytes accessed | tf_op | source)
XLA Modules:
  0.0 45.6 jit_solution(17230888699797325820)
XLA Ops:
  0.7 0.8 %dynamic-slice_bitcast_fusion = (bf16[1,2,16,512]{3,2,1,0:T(8,128)(2,1)S(1)}, bf16[2,16,512]{2,1,0:T(8,128)(2,1)S(1)}, bf16[2,16,512]{2,1,0:T(8,128)(2,1)S(1)}, bf16[2,16,512]{2,1,0:T(8,128)(2,1)S(1)}) fusion(bf16[2,16,2048]{2,1,0:T(8,128)(2,1)} %param.5, s32[]{:T(128)S(6)} %select_n.12, s32[]{:T(128)S(6)} %select_n.13, s32[]{:T(128)S(6)} %select_n.15, ...), kind=kLoop, calls=%fused_computation.2 | loop fusion | bytes 262160 | tf_op jit(solution)/shard_map/stack | solution.py:199
  1.5 0.6 %collective-permute-start = (bf16[2,16,512]{2,1,0:T(8,128)(2,1)S(1)}, bf16[2,16,512]{2,1,0:T(8,128)(2,1)S(1)}, u32[]{:S(2)}, u32[]{:S(2)}) collective-permute-start(bf16[2,16,512]{2,1,0:T(8,128)(2,1)S(1)} %get-tuple-element.3), channel_id=1, source_target_pairs={{0,1},{1,0},{2,3},{3,2},{4,5},{5,4},{6,7},{7,6},{8,9},{9,8},{10,11... | collective-permute-start | bytes 98312 | tf_op jit(solution)/shard_map/ppermute | solution.py:198
  2.0 2.6 %collective-permute-start.2 = (bf16[2,16,512]{2,1,0:T(8,128)(2,1)S(1)}, bf16[2,16,512]{2,1,0:T(8,128)(2,1)S(1)}, u32[]{:S(2)}, u32[]{:S(2)}) collective-permute-start(bf16[2,16,512]{2,1,0:T(8,128)(2,1)S(1)} %get-tuple-element.4), channel_id=1, source_target_pairs={{0,3},{1,2},{2,1},{3,0},{4,7},{5,6},{6,5},{7,4},{8,11},{9,10},{10,... | collective-permute-start | bytes 98312 | tf_op jit(solution)/shard_map/ppermute | solution.py:198
  4.6 0.0 collective-permute-start.1
  4.7 4.1 %collective-permute-start.12 = (bf16[1,2,64,128]{3,2,1,0:T(8,128)(2,1)}, bf16[1,2,64,128]{3,2,1,0:T(8,128)(2,1)S(1)}, u32[]{:S(2)}, u32[]{:S(2)}) collective-permute-start(bf16[1,2,64,128]{3,2,1,0:T(8,128)(2,1)} %bitcast.8), channel_id=1, source_target_pairs={{0,24},{4,28},{8,16},{12,20},{16,8},{20,12},{24,0},{28,4},{1,25},{... | collective-permute-start | bytes 98312 | tf_op jit(solution)/shard_map/ppermute | solution.py:209
  8.8 0.0 collective-permute-start.11
  8.8 0.0 collective-permute-done
  8.8 0.6 %collective-permute-start.10 = (bf16[1,2,64,128]{3,2,1,0:T(8,128)(2,1)}, bf16[1,2,64,128]{3,2,1,0:T(8,128)(2,1)S(1)}, u32[]{:S(2)}, u32[]{:S(2)}) collective-permute-start(bf16[1,2,64,128]{3,2,1,0:T(8,128)(2,1)} %bitcast.10), channel_id=1, source_target_pairs={{0,8},{4,12},{8,0},{12,4},{16,24},{20,28},{24,16},{28,20},{1,9},{5... | collective-permute-start | bytes 98312 | tf_op jit(solution)/shard_map/ppermute | solution.py:209
  9.3 0.0 collective-permute-done.2
  9.3 0.0 collective-permute-done.1
  9.4 1.8 %collective-permute-start.6 = (bf16[4,2,16,512]{3,2,1,0:T(8,128)(2,1)S(1)}, bf16[4,2,16,512]{3,2,1,0:T(8,128)(2,1)S(1)}, u32[]{:S(2)}, u32[]{:S(2)}) collective-permute-start(bf16[4,2,16,512]{3,2,1,0:T(8,128)(2,1)S(1)} %pad_maximum_fusion.refs_0_), channel_id=1, source_target_pairs={{0,4},{4,0},{8,12},{12,8},{16,20},{20,16},{24,28},{28,24},{1,5},{5... | collective-permute-start | bytes 393224 | tf_op jit(solution)/shard_map/ppermute | solution.py:203
  11.2 3.6 %collective-permute-start.5 = (bf16[4,2,16,512]{3,2,1,0:T(8,128)(2,1)S(1)}, bf16[4,2,16,512]{3,2,1,0:T(8,128)(2,1)S(1)}, u32[]{:S(2)}, u32[]{:S(2)}) collective-permute-start(bf16[4,2,16,512]{3,2,1,0:T(8,128)(2,1)S(1)} %pad_maximum_fusion.refs_0_), channel_id=1, source_target_pairs={{0,24},{4,28},{8,16},{12,20},{16,8},{20,12},{24,0},{28,4},{1,25},{... | collective-permute-start | bytes 393224 | tf_op jit(solution)/shard_map/ppermute | solution.py:201
  14.8 0.0 collective-permute-done.12
  14.8 0.0 collective-permute-start.4
  14.8 0.0 collective-permute-done.11
  14.8 0.0 collective-permute-done.10
  14.8 0.8 %pad_maximum_fusion.1.refs_8_ = bf16[4,2,64,128]{3,2,1,0:T(8,128)(2,1)S(1)} fusion(bf16[1,2,64,128]{3,2,1,0:T(8,128)(2,1)S(1)} %collective-permute-done.12, bf16[1,2,64,128]{3,2,1,0:T(8,128)(2,1)S(1)} %collective-permute-done.11, bf16[1,2,64,128]{3,2,1,0:T(8,128)(2,1)S(1)} %collective-permute-done.10, bf16[1,2,64,128]{3,2,1,0:T(8,128)(2,1)} %bitcast.11), kind=kLoop, calls=%fused_computation.1 | loop fusion | flops 196608 | bytes 262144 | tf_op jit(solution)/shard_map/concatenate | solution.py:207
  15.6 6.2 %collective-permute-start.13 = (bf16[4,2,64,128]{3,2,1,0:T(8,128)(2,1)S(1)}, bf16[4,2,64,128]{3,2,1,0:T(8,128)(2,1)S(1)}, u32[]{:S(2)}, u32[]{:S(2)}) collective-permute-start(bf16[4,2,64,128]{3,2,1,0:T(8,128)(2,1)S(1)} %pad_maximum_fusion.1.refs_8_), channel_id=1, source_target_pairs={{0,4},{4,0},{8,12},{12,8},{16,20},{20,16},{24,28},{28,24},{1,5},{5... | collective-permute-start | bytes 393224 | tf_op jit(solution)/shard_map/ppermute | solution.py:211
  21.7 0.0 collective-permute-start.3
  21.7 0.0 collective-permute-done.6.refs_4_
  21.7 0.0 collective-permute-start.16
  21.8 0.0 collective-permute-done.5.refs_3_
  21.8 1.6 %collective-permute-start.14 = (bf16[4,2,64,128]{3,2,1,0:T(8,128)(2,1)S(1)}, bf16[4,2,64,128]{3,2,1,0:T(8,128)(2,1)S(1)}, u32[]{:S(2)}, u32[]{:S(2)}) collective-permute-start(bf16[4,2,64,128]{3,2,1,0:T(8,128)(2,1)S(1)} %pad_maximum_fusion.1.refs_8_), channel_id=1, source_target_pairs={{0,2},{1,3},{2,0},{3,1},{4,6},{5,7},{6,4},{7,5},{8,10},{9,11},{10,... | collective-permute-start | bytes 393224 | tf_op jit(solution)/shard_map/ppermute | solution.py:215
  23.3 1.7 %collective-permute-done.4.refs_2_ = bf16[4,2,16,512]{3,2,1,0:T(8,128)(2,1)S(1)} collective-permute-done((bf16[4,2,16,512]{3,2,1,0:T(8,128)(2,1)S(1)}, bf16[4,2,16,512]{3,2,1,0:T(8,128)(2,1)S(1)}, u32[]{:S(2)}, u32[]{:S(2)}) %collective-permute-start.4) | collective-permute-done | bytes 131104 | tf_op jit(solution)/shard_map/ppermute | solution.py:201
  25.0 0.9 %collective-permute-start.9 = (bf16[4,2,16,512]{3,2,1,0:T(8,128)(2,1)S(1)}, bf16[4,2,16,512]{3,2,1,0:T(8,128)(2,1)S(1)}, u32[]{:S(2)}, u32[]{:S(2)}) collective-permute-start(bf16[4,2,16,512]{3,2,1,0:T(8,128)(2,1)S(1)} %collective-permute-done.5.refs_3_), channel_id=1, source_target_pairs={{0,4},{4,0},{8,12},{12,8},{16,20},{20,16},{24,28},{28,24},{1,5},{5... | collective-permute-start | bytes 393224 | tf_op jit(solution)/shard_map/ppermute | solution.py:203
  25.9 0.0 collective-permute-done.13.refs_9_
  25.9 1.5 %collective-permute-start.15 = (bf16[4,2,64,128]{3,2,1,0:T(8,128)(2,1)S(1)}, bf16[4,2,64,128]{3,2,1,0:T(8,128)(2,1)S(1)}, u32[]{:S(2)}, u32[]{:S(2)}) collective-permute-start(bf16[4,2,64,128]{3,2,1,0:T(8,128)(2,1)S(1)} %collective-permute-done.13.refs_9_), channel_id=1, source_target_pairs={{0,2},{1,3},{2,0},{3,1},{4,6},{5,7},{6,4},{7,5},{8,10},{9,11},{10,... | collective-permute-start | bytes 393224 | tf_op jit(solution)/shard_map/ppermute | solution.py:215
  27.4 0.0 collective-permute-done.3.refs_1_
  27.4 0.0 collective-permute-start.17
  27.4 0.0 collective-permute-done.16.refs_12_
  27.4 1.2 %collective-permute-start.8 = (bf16[4,2,16,512]{3,2,1,0:T(8,128)(2,1)S(1)}, bf16[4,2,16,512]{3,2,1,0:T(8,128)(2,1)S(1)}, u32[]{:S(2)}, u32[]{:S(2)}) collective-permute-start(bf16[4,2,16,512]{3,2,1,0:T(8,128)(2,1)S(1)} %collective-permute-done.4.refs_2_), channel_id=1, source_target_pairs={{0,4},{4,0},{8,12},{12,8},{16,20},{20,16},{24,28},{28,24},{1,5},{5... | collective-permute-start | bytes 393224 | tf_op jit(solution)/shard_map/ppermute | solution.py:203
  28.6 0.0 collective-permute-done.14.refs_10_
  28.6 0.9 %collective-permute-start.7 = (bf16[4,2,16,512]{3,2,1,0:T(8,128)(2,1)S(1)}, bf16[4,2,16,512]{3,2,1,0:T(8,128)(2,1)S(1)}, u32[]{:S(2)}, u32[]{:S(2)}) collective-permute-start(bf16[4,2,16,512]{3,2,1,0:T(8,128)(2,1)S(1)} %collective-permute-done.3.refs_1_), channel_id=1, source_target_pairs={{0,4},{4,0},{8,12},{12,8},{16,20},{20,16},{24,28},{28,24},{1,5},{5... | collective-permute-start | bytes 393224 | tf_op jit(solution)/shard_map/ppermute | solution.py:203
  29.5 0.5 %collective-permute-done.9.refs_7_ = bf16[4,2,16,512]{3,2,1,0:T(8,128)(2,1)S(1)} collective-permute-done((bf16[4,2,16,512]{3,2,1,0:T(8,128)(2,1)S(1)}, bf16[4,2,16,512]{3,2,1,0:T(8,128)(2,1)S(1)}, u32[]{:S(2)}, u32[]{:S(2)}) %collective-permute-start.9) | collective-permute-done | bytes 131104 | tf_op jit(solution)/shard_map/ppermute | solution.py:203
  30.0 0.0 collective-permute-start.18
  30.0 0.9 %collective-permute-done.15.refs_11_ = bf16[4,2,64,128]{3,2,1,0:T(8,128)(2,1)S(1)} collective-permute-done((bf16[4,2,64,128]{3,2,1,0:T(8,128)(2,1)S(1)}, bf16[4,2,64,128]{3,2,1,0:T(8,128)(2,1)S(1)}, u32[]{:S(2)}, u32[]{:S(2)}) %collective-permute-start.15) | collective-permute-done | bytes 131104 | tf_op jit(solution)/shard_map/ppermute | solution.py:215
  30.9 0.0 collective-permute-start.19
  30.9 3.0 %collective-permute-done.8.refs_6_ = bf16[4,2,16,512]{3,2,1,0:T(8,128)(2,1)S(1)} collective-permute-done((bf16[4,2,16,512]{3,2,1,0:T(8,128)(2,1)S(1)}, bf16[4,2,16,512]{3,2,1,0:T(8,128)(2,1)S(1)}, u32[]{:S(2)}, u32[]{:S(2)}) %collective-permute-start.8) | collective-permute-done | bytes 131104 | tf_op jit(solution)/shard_map/ppermute | solution.py:203
  33.8 2.3 %collective-permute-done.7.refs_5_ = bf16[4,2,16,512]{3,2,1,0:T(8,128)(2,1)S(1)} collective-permute-done((bf16[4,2,16,512]{3,2,1,0:T(8,128)(2,1)S(1)}, bf16[4,2,16,512]{3,2,1,0:T(8,128)(2,1)S(1)}, u32[]{:S(2)}, u32[]{:S(2)}) %collective-permute-start.7) | collective-permute-done | bytes 131104 | tf_op jit(solution)/shard_map/ppermute | solution.py:203
  36.1 0.0 collective-permute-done.18.refs_14_
  36.1 0.0 collective-permute-done.17.refs_13_
  36.1 0.0 collective-permute-done.19.refs_15_
  36.1 9.5 %finish.1 = (bf16[2,64,512]{2,1,0:T(8,128)(2,1)}, f32[2,512,512]{2,1,0:T(8,128)}) custom-call(s32[1]{0:T(128)} %bitcast.row_ref, s32[1]{0:T(128)} %bitcast.1.col_ref, s32[1,4]{1,0:T(1,128)} %pattern_ref.1, bf16[4,2,16,512]{3,2,1,0:T(8,128)(2,1)S(1)} %pad_maximum_fusion.refs_0_, bf16[4,2,16,512]{3,2,1,0:T(8,128)(2,1)S(1)} %collective-permute-done.3.refs_1_, ...), custom_call_target="tpu_custom_call" | custom-call | tf_op jit(solution)/shard_map/finish/pallas_call | solution.py:236
  (1 shorter events, 0.0 us)
Async XLA Ops:
  1.5 7.3 %collective-permute-start = (bf16[2,16,512]{2,1,0:T(8,128)(2,1)S(1)}, bf16[2,16,512]{2,1,0:T(8,128)(2,1)S(1)}, u32[]{:S(2)}, u32[]{:S(2)}) collective-permute-start(bf16[2,16,512]{2,1,0:T(8,128)(2,1)S(1)} %get-tuple-element.3), channel_id=1, source_target_pairs={{0,1},{1,0},{2,3},{3,2},{4,5},{5,4},{6,7},{7,6},{8,9},{9,8},{10,11... | collective-permute-start | bytes 98312 | tf_op jit(solution)/shard_map/ppermute | solution.py:198
  2.0 7.3 %collective-permute-start.2 = (bf16[2,16,512]{2,1,0:T(8,128)(2,1)S(1)}, bf16[2,16,512]{2,1,0:T(8,128)(2,1)S(1)}, u32[]{:S(2)}, u32[]{:S(2)}) collective-permute-start(bf16[2,16,512]{2,1,0:T(8,128)(2,1)S(1)} %get-tuple-element.4), channel_id=1, source_target_pairs={{0,3},{1,2},{2,1},{3,0},{4,7},{5,6},{6,5},{7,4},{8,11},{9,10},{10,... | collective-permute-start | bytes 98312 | tf_op jit(solution)/shard_map/ppermute | solution.py:198
  4.6 4.7 %collective-permute-start.1 = (bf16[2,16,512]{2,1,0:T(8,128)(2,1)S(1)}, bf16[2,16,512]{2,1,0:T(8,128)(2,1)S(1)}, u32[]{:S(2)}, u32[]{:S(2)}) collective-permute-start(bf16[2,16,512]{2,1,0:T(8,128)(2,1)S(1)} %get-tuple-element.5), channel_id=1, source_target_pairs={{0,2},{1,3},{2,0},{3,1},{4,6},{5,7},{6,4},{7,5},{8,10},{9,11},{10,... | collective-permute-start | bytes 98312 | tf_op jit(solution)/shard_map/ppermute | solution.py:198
  4.7 10.1 %collective-permute-start.12 = (bf16[1,2,64,128]{3,2,1,0:T(8,128)(2,1)}, bf16[1,2,64,128]{3,2,1,0:T(8,128)(2,1)S(1)}, u32[]{:S(2)}, u32[]{:S(2)}) collective-permute-start(bf16[1,2,64,128]{3,2,1,0:T(8,128)(2,1)} %bitcast.8), channel_id=1, source_target_pairs={{0,24},{4,28},{8,16},{12,20},{16,8},{20,12},{24,0},{28,4},{1,25},{... | collective-permute-start | bytes 98312 | tf_op jit(solution)/shard_map/ppermute | solution.py:209
  8.8 6.0 %collective-permute-start.11 = (bf16[1,2,64,128]{3,2,1,0:T(8,128)(2,1)}, bf16[1,2,64,128]{3,2,1,0:T(8,128)(2,1)S(1)}, u32[]{:S(2)}, u32[]{:S(2)}) collective-permute-start(bf16[1,2,64,128]{3,2,1,0:T(8,128)(2,1)} %bitcast.9), channel_id=1, source_target_pairs={{0,16},{4,20},{8,24},{12,28},{16,0},{20,4},{24,8},{28,12},{1,17},{... | collective-permute-start | bytes 98312 | tf_op jit(solution)/shard_map/ppermute | solution.py:209
  8.8 6.0 %collective-permute-start.10 = (bf16[1,2,64,128]{3,2,1,0:T(8,128)(2,1)}, bf16[1,2,64,128]{3,2,1,0:T(8,128)(2,1)S(1)}, u32[]{:S(2)}, u32[]{:S(2)}) collective-permute-start(bf16[1,2,64,128]{3,2,1,0:T(8,128)(2,1)} %bitcast.10), channel_id=1, source_target_pairs={{0,8},{4,12},{8,0},{12,4},{16,24},{20,28},{24,16},{28,20},{1,9},{5... | collective-permute-start | bytes 98312 | tf_op jit(solution)/shard_map/ppermute | solution.py:209
  9.4 12.4 %collective-permute-start.6 = (bf16[4,2,16,512]{3,2,1,0:T(8,128)(2,1)S(1)}, bf16[4,2,16,512]{3,2,1,0:T(8,128)(2,1)S(1)}, u32[]{:S(2)}, u32[]{:S(2)}) collective-permute-start(bf16[4,2,16,512]{3,2,1,0:T(8,128)(2,1)S(1)} %pad_maximum_fusion.refs_0_), channel_id=1, source_target_pairs={{0,4},{4,0},{8,12},{12,8},{16,20},{20,16},{24,28},{28,24},{1,5},{5... | collective-permute-start | bytes 393224 | tf_op jit(solution)/shard_map/ppermute | solution.py:203
  11.2 10.6 %collective-permute-start.5 = (bf16[4,2,16,512]{3,2,1,0:T(8,128)(2,1)S(1)}, bf16[4,2,16,512]{3,2,1,0:T(8,128)(2,1)S(1)}, u32[]{:S(2)}, u32[]{:S(2)}) collective-permute-start(bf16[4,2,16,512]{3,2,1,0:T(8,128)(2,1)S(1)} %pad_maximum_fusion.refs_0_), channel_id=1, source_target_pairs={{0,24},{4,28},{8,16},{12,20},{16,8},{20,12},{24,0},{28,4},{1,25},{... | collective-permute-start | bytes 393224 | tf_op jit(solution)/shard_map/ppermute | solution.py:201
  14.8 10.2 %collective-permute-start.4 = (bf16[4,2,16,512]{3,2,1,0:T(8,128)(2,1)S(1)}, bf16[4,2,16,512]{3,2,1,0:T(8,128)(2,1)S(1)}, u32[]{:S(2)}, u32[]{:S(2)}) collective-permute-start(bf16[4,2,16,512]{3,2,1,0:T(8,128)(2,1)S(1)} %pad_maximum_fusion.refs_0_), channel_id=1, source_target_pairs={{0,16},{4,20},{8,24},{12,28},{16,0},{20,4},{24,8},{28,12},{1,17},{... | collective-permute-start | bytes 393224 | tf_op jit(solution)/shard_map/ppermute | solution.py:201
  15.6 10.3 %collective-permute-start.13 = (bf16[4,2,64,128]{3,2,1,0:T(8,128)(2,1)S(1)}, bf16[4,2,64,128]{3,2,1,0:T(8,128)(2,1)S(1)}, u32[]{:S(2)}, u32[]{:S(2)}) collective-permute-start(bf16[4,2,64,128]{3,2,1,0:T(8,128)(2,1)S(1)} %pad_maximum_fusion.1.refs_8_), channel_id=1, source_target_pairs={{0,4},{4,0},{8,12},{12,8},{16,20},{20,16},{24,28},{28,24},{1,5},{5... | collective-permute-start | bytes 393224 | tf_op jit(solution)/shard_map/ppermute | solution.py:211
  21.7 5.7 %collective-permute-start.3 = (bf16[4,2,16,512]{3,2,1,0:T(8,128)(2,1)S(1)}, bf16[4,2,16,512]{3,2,1,0:T(8,128)(2,1)S(1)}, u32[]{:S(2)}, u32[]{:S(2)}) collective-permute-start(bf16[4,2,16,512]{3,2,1,0:T(8,128)(2,1)S(1)} %pad_maximum_fusion.refs_0_), channel_id=1, source_target_pairs={{0,8},{4,12},{8,0},{12,4},{16,24},{20,28},{24,16},{28,20},{1,9},{5... | collective-permute-start | bytes 393224 | tf_op jit(solution)/shard_map/ppermute | solution.py:201
  21.7 5.7 %collective-permute-start.16 = (bf16[4,2,64,128]{3,2,1,0:T(8,128)(2,1)S(1)}, bf16[4,2,64,128]{3,2,1,0:T(8,128)(2,1)S(1)}, u32[]{:S(2)}, u32[]{:S(2)}) collective-permute-start(bf16[4,2,64,128]{3,2,1,0:T(8,128)(2,1)S(1)} %pad_maximum_fusion.1.refs_8_), channel_id=1, source_target_pairs={{0,1},{1,0},{2,3},{3,2},{4,5},{5,4},{6,7},{7,6},{8,9},{9,8},{10,11... | collective-permute-start | bytes 393224 | tf_op jit(solution)/shard_map/ppermute | solution.py:216
  21.8 6.8 %collective-permute-start.14 = (bf16[4,2,64,128]{3,2,1,0:T(8,128)(2,1)S(1)}, bf16[4,2,64,128]{3,2,1,0:T(8,128)(2,1)S(1)}, u32[]{:S(2)}, u32[]{:S(2)}) collective-permute-start(bf16[4,2,64,128]{3,2,1,0:T(8,128)(2,1)S(1)} %pad_maximum_fusion.1.refs_8_), channel_id=1, source_target_pairs={{0,2},{1,3},{2,0},{3,1},{4,6},{5,7},{6,4},{7,5},{8,10},{9,11},{10,... | collective-permute-start | bytes 393224 | tf_op jit(solution)/shard_map/ppermute | solution.py:215
  25.0 5.0 %collective-permute-start.9 = (bf16[4,2,16,512]{3,2,1,0:T(8,128)(2,1)S(1)}, bf16[4,2,16,512]{3,2,1,0:T(8,128)(2,1)S(1)}, u32[]{:S(2)}, u32[]{:S(2)}) collective-permute-start(bf16[4,2,16,512]{3,2,1,0:T(8,128)(2,1)S(1)} %collective-permute-done.5.refs_3_), channel_id=1, source_target_pairs={{0,4},{4,0},{8,12},{12,8},{16,20},{20,16},{24,28},{28,24},{1,5},{5... | collective-permute-start | bytes 393224 | tf_op jit(solution)/shard_map/ppermute | solution.py:203
  25.9 5.0 %collective-permute-start.15 = (bf16[4,2,64,128]{3,2,1,0:T(8,128)(2,1)S(1)}, bf16[4,2,64,128]{3,2,1,0:T(8,128)(2,1)S(1)}, u32[]{:S(2)}, u32[]{:S(2)}) collective-permute-start(bf16[4,2,64,128]{3,2,1,0:T(8,128)(2,1)S(1)} %collective-permute-done.13.refs_9_), channel_id=1, source_target_pairs={{0,2},{1,3},{2,0},{3,1},{4,6},{5,7},{6,4},{7,5},{8,10},{9,11},{10,... | collective-permute-start | bytes 393224 | tf_op jit(solution)/shard_map/ppermute | solution.py:215
  27.4 8.7 %collective-permute-start.17 = (bf16[4,2,64,128]{3,2,1,0:T(8,128)(2,1)S(1)}, bf16[4,2,64,128]{3,2,1,0:T(8,128)(2,1)S(1)}, u32[]{:S(2)}, u32[]{:S(2)}) collective-permute-start(bf16[4,2,64,128]{3,2,1,0:T(8,128)(2,1)S(1)} %collective-permute-done.13.refs_9_), channel_id=1, source_target_pairs={{0,1},{1,0},{2,3},{3,2},{4,5},{5,4},{6,7},{7,6},{8,9},{9,8},{10,11... | collective-permute-start | bytes 393224 | tf_op jit(solution)/shard_map/ppermute | solution.py:216
  27.4 6.4 %collective-permute-start.8 = (bf16[4,2,16,512]{3,2,1,0:T(8,128)(2,1)S(1)}, bf16[4,2,16,512]{3,2,1,0:T(8,128)(2,1)S(1)}, u32[]{:S(2)}, u32[]{:S(2)}) collective-permute-start(bf16[4,2,16,512]{3,2,1,0:T(8,128)(2,1)S(1)} %collective-permute-done.4.refs_2_), channel_id=1, source_target_pairs={{0,4},{4,0},{8,12},{12,8},{16,20},{20,16},{24,28},{28,24},{1,5},{5... | collective-permute-start | bytes 393224 | tf_op jit(solution)/shard_map/ppermute | solution.py:203
  28.6 7.5 %collective-permute-start.7 = (bf16[4,2,16,512]{3,2,1,0:T(8,128)(2,1)S(1)}, bf16[4,2,16,512]{3,2,1,0:T(8,128)(2,1)S(1)}, u32[]{:S(2)}, u32[]{:S(2)}) collective-permute-start(bf16[4,2,16,512]{3,2,1,0:T(8,128)(2,1)S(1)} %collective-permute-done.3.refs_1_), channel_id=1, source_target_pairs={{0,4},{4,0},{8,12},{12,8},{16,20},{20,16},{24,28},{28,24},{1,5},{5... | collective-permute-start | bytes 393224 | tf_op jit(solution)/shard_map/ppermute | solution.py:203
  30.0 6.2 %collective-permute-start.18 = (bf16[4,2,64,128]{3,2,1,0:T(8,128)(2,1)S(1)}, bf16[4,2,64,128]{3,2,1,0:T(8,128)(2,1)S(1)}, u32[]{:S(2)}, u32[]{:S(2)}) collective-permute-start(bf16[4,2,64,128]{3,2,1,0:T(8,128)(2,1)S(1)} %collective-permute-done.14.refs_10_), channel_id=1, source_target_pairs={{0,1},{1,0},{2,3},{3,2},{4,5},{5,4},{6,7},{7,6},{8,9},{9,8},{10,11... | collective-permute-start | bytes 393224 | tf_op jit(solution)/shard_map/ppermute | solution.py:216
  30.9 5.3 %collective-permute-start.19 = (bf16[4,2,64,128]{3,2,1,0:T(8,128)(2,1)S(1)}, bf16[4,2,64,128]{3,2,1,0:T(8,128)(2,1)S(1)}, u32[]{:S(2)}, u32[]{:S(2)}) collective-permute-start(bf16[4,2,64,128]{3,2,1,0:T(8,128)(2,1)S(1)} %collective-permute-done.15.refs_11_), channel_id=1, source_target_pairs={{0,1},{1,0},{2,3},{3,2},{4,5},{5,4},{6,7},{7,6},{8,9},{9,8},{10,11... | collective-permute-start | bytes 393224 | tf_op jit(solution)/shard_map/ppermute | solution.py:216
